TPU v7x, 256 devices: a whole 4x4x8 slice. The times are simulated.
256 devices in a mesh: expert: 128 (over x_hi, y, z, core), tensor: 2 (over x_lo).
Axes of the slice: x: 4 (x_hi: 2, x_lo: 2; x = x_hi * 2 + x_lo), y: 4, z: 8, core: 2. Of those that a mesh axis runs over, the one named last changes fastest.
Arguments:
- tokens: bfloat16 [65536, 768], P(('expert', 'tensor')), may hold values from -6 to 6
- norm_gain: float32 [768], replicated, may hold values from 0.25 to 1.75
- gates: float32 [65536], P(('expert', 'tensor')), may hold values from 0.25 to 1
- expert_ids: int32 [65536], P(('expert', 'tensor')), may hold values from 0 to 255, as said below
- slots: int32 [65536], P(('expert', 'tensor')), may hold values from -1 to 1, as said below
- w_in: bfloat16 [256, 768, 3072], P(('expert', 'tensor')), may hold values from -0.21875 to 0.21875
- w_out: bfloat16 [256, 768, 3072], P(('expert', 'tensor')), may hold values from -0.109375 to 0.109375
Outputs:
- mixed: bfloat16 [65536, 768], P(('expert', 'tensor'))
Inputs may be any that keep to these rules, and one draw needn't show every extreme that they name: `expert_ids`: each token's expert, 0 to 255; in every block of 256 tokens one expert, the same in all blocks, is chosen by 2 + 1 or more tokens at positions that differ from block to block. `slots`: the slot of a token is the number of earlier tokens of its block of 256 that chose the same expert, if that is below 2, else -1; so at most 2 tokens of one block reach one expert, and one expert receives exactly 2 from every block.
All inputs are finite; a program needn't handle non-finite values.
Results may differ from a plain program's by a relative error of at most 0.0037.
Values may be sent and summed in bfloat16 or wider, within the bound.
No kernel may reach another device: no remote copies, remote signals or barrier semaphores. Data moves between devices by JAX's collectives and lax.ppermute only.
A program may use at most 64 MiB of HBM per device.

v0:
```python
import jax
import jax.numpy as jnp
from jax import lax
from jax.sharding import PartitionSpec as P


def cut_along(array, dim, size):
    lengths = array.shape
    blocks = array.reshape(*lengths[:dim], size, lengths[dim] // size, *lengths[dim + 1 :])
    return jnp.moveaxis(blocks, dim, 0)


def in_order(blocks, dim):
    blocks = jnp.moveaxis(blocks, 0, dim)
    lengths = blocks.shape
    return blocks.reshape(*lengths[:dim], lengths[dim] * lengths[dim + 1], *lengths[dim + 2 :])


def joined_exchange(array, axis, axes, splits, concats):
    sizes = [lax.axis_size(a) for a in axes]
    blocks = cut_along(array, splits[0], sizes[0])
    blocks = jnp.moveaxis(cut_along(blocks, splits[1] + 1, sizes[1]), 0, 1)
    inside = blocks.shape[2:]
    blocks = blocks.reshape(-1, *inside)
    blocks = lax.all_to_all(blocks, axis, split_axis=0, concat_axis=0, tiled=True)
    blocks = in_order(blocks.reshape(*sizes, *inside), concats[0] + 1)
    return in_order(blocks, concats[1])


def slot_mask(expert_ids, slots, experts, capacity):
    index = expert_ids * capacity + slots
    columns = jnp.arange(experts * capacity, dtype=jnp.int32)
    valid = slots >= 0
    return ((index[:, None] == columns[None, :]) & valid[:, None]).astype(jnp.bfloat16)


def normalize(tokens, norm_gain):
    values = tokens.astype(jnp.float32)
    square = jnp.mean(values * values, axis=-1, keepdims=True)
    return (values * lax.rsqrt(square + 1e-06) * norm_gain[None, :]).astype(jnp.bfloat16)


def local(tokens, norm_gain, gates, expert_ids, slots, w_in, w_out):
    tok_dev, width = tokens.shape
    n_expert = lax.axis_size("expert")
    n_tensor = lax.axis_size("tensor")
    experts = n_expert * n_tensor
    capacity = max(2, 2 * tok_dev // experts)
    normed = normalize(tokens, norm_gain)
    masked = slot_mask(expert_ids, slots, experts, capacity)
    buffer = jnp.dot(masked.T, normed, preferred_element_type=jnp.float32).astype(jnp.bfloat16)
    sent = buffer.reshape(n_expert, n_tensor, capacity, width)
    arrived = joined_exchange(sent, ("expert", "tensor"), ("expert", "tensor"), (0, 1), (0, 1))
    rows = arrived.reshape(experts * capacity, width)
    hidden = jnp.maximum(jnp.dot(rows, w_in[0], preferred_element_type=jnp.float32), 0.0).astype(
        jnp.bfloat16
    )
    result = lax.dot_general(
        hidden, w_out[0], (((1,), (1,)), ((), ())), preferred_element_type=jnp.float32
    )
    result = result.astype(jnp.bfloat16).reshape(n_expert, n_tensor, capacity, width)
    returned = joined_exchange(result, ("expert", "tensor"), ("expert", "tensor"), (0, 1), (0, 1))
    picked = jnp.dot(
        masked, returned.reshape(experts * capacity, width), preferred_element_type=jnp.float32
    )
    return (tokens.astype(jnp.float32) + gates[:, None] * picked).astype(jnp.bfloat16)


def solution(mesh):
    in_specs = (
        P(("expert", "tensor"), None),
        P(),
        P(("expert", "tensor")),
        P(("expert", "tensor")),
        P(("expert", "tensor")),
        P(("expert", "tensor"), None, None),
        P(("expert", "tensor"), None, None),
    )
    out_specs = P(("expert", "tensor"), None)
    return jax.shard_map(local, mesh=mesh, in_specs=in_specs, out_specs=out_specs, check_vma=False)
```

profile of v0, /device:TPU:1, one launch (start us, length us, event | category | flops | bytes accessed | tf_op | source)
XLA Modules:
  0.0 89.0 jit_solution(15588611518067541169)
XLA Ops:
  0.0 0.7 broadcast_compare_fusion
  0.7 0.7 multiply_add_fusion
  1.4 1.2 %fusion.8 = f32[256]{0:T(256)S(1)} fusion(bf16[256,768]{1,0:T(8,128)(2,1)} %param.7), kind=kLoop, calls=%fused_computation.11 | loop fusion | flops 589568 | bytes 394240 | tf_op jit(solution)/shard_map/reduce_sum | solution.py:39
  2.5 1.6 %convolution_convert_fusion = bf16[512,768]{1,0:T(8,128)(2,1)S(1)} fusion(bf16[256,768]{1,0:T(8,128)(2,1)} %param.7, f32[768]{0:T(1024)} %param.8, f32[256]{0:T(256)S(1)} %add_rsqrt_fusion, s32[256]{0:T(256)S(1)} %multiply_add_fusion, pred[256]{0:T(512)(128)(4,1)S(1)} %broadcast_compare_fusion), kind=kOutput, calls=%fused_computation.5 | convolution fusion | flops 202768384 | bytes 1185024 | tf_op jit(solution)/shard_map/dot_general | solution.py:51
  4.2 0.3 reshape_transpose_transpose_reshape_reshape_reshape.6
  4.5 40.9 %all_to_all.10 = bf16[256,1,1,2,768]{4,3,2,1,0:T(2,128)(2,1)S(1)} all-to-all(bf16[256,1,1,2,768]{4,3,2,1,0:T(2,128)(2,1)S(1)} %bitcast.31), channel_id=1, replica_groups=mesh['expert'=128,'tensor'=2] {'expert','tensor'}, dimensions={0} | all-to-all | bytes 1572864 | tf_op jit(solution)/shard_map/all_to_all | solution.py:25
  45.3 0.3 reshape_reshape.6
  45.6 5.2 %maximum_convert_fusion = bf16[512,3072]{1,0:T(8,128)(2,1)S(1)} fusion(bf16[512,768]{1,0:T(8,128)(2,1)S(1)} %reshape_reshape.6, bf16[1,768,3072]{2,1,0:T(8,128)(2,1)} %param.12), kind=kOutput, calls=%fused_computation | convolution fusion | flops 2419064832 | bytes 8650752 | tf_op jit(solution)/shard_map/dot_general | solution.py:55
  50.9 5.0 %fusion.3 = bf16[512,768]{1,0:T(8,128)(2,1)S(1)} fusion(bf16[512,3072]{1,0:T(8,128)(2,1)S(1)} %maximum_convert_fusion, bf16[1,768,3072]{2,1,0:T(8,128)(2,1)} %param.13), kind=kOutput, calls=%fused_computation.4 | convolution fusion | flops 2416312320 | bytes 8650752 | tf_op jit(solution)/shard_map/dot_general | solution.py:58
  55.9 0.0 copy-start
  55.9 0.0 copy-start.1
  55.9 0.3 reshape_transpose_transpose_reshape_reshape_reshape.7
  56.2 31.3 %all_to_all.11 = bf16[256,1,1,2,768]{4,3,2,1,0:T(2,128)(2,1)S(1)} all-to-all(bf16[256,1,1,2,768]{4,3,2,1,0:T(2,128)(2,1)S(1)} %bitcast.33), channel_id=1, replica_groups=mesh['expert'=128,'tensor'=2] {'expert','tensor'}, dimensions={0} | all-to-all | bytes 1572864 | tf_op jit(solution)/shard_map/all_to_all | solution.py:25
  87.5 0.3 reshape_reshape.7
  87.8 0.0 copy-done
  87.8 0.0 copy-done.1
  87.8 1.2 %fusion.7 = bf16[256,768]{1,0:T(8,128)(2,1)} fusion(bf16[512,768]{1,0:T(8,128)(2,1)S(1)} %reshape_reshape.7, bf16[256,768]{1,0:T(8,128)(2,1)S(1)} %copy-done, f32[256]{0:T(256)S(1)} %copy-done.1, s32[256]{0:T(256)S(1)} %multiply_add_fusion, pred[256]{0:T(512)(128)(4,1)S(1)} %broadcast_compare_fusion), kind=kOutput, calls=%fused_computation.8 | convolution fusion | flops 202375168 | bytes 1575168 | tf_op jit(solution)/shard_map/dot_general | solution.py:63
  (1 shorter events, 0.0 us)
Async XLA Ops:
  55.9 31.9 %copy-start = (bf16[256,768]{1,0:T(8,128)(2,1)S(1)}, bf16[256,768]{1,0:T(8,128)(2,1)}, u32[]{:S(2)}) copy-start(bf16[256,768]{1,0:T(8,128)(2,1)} %param.7) | copy-start | bytes 1179652
  55.9 31.9 %copy-start.1 = (f32[256]{0:T(256)S(1)}, f32[256]{0:T(256)}, u32[]{:S(2)}) copy-start(f32[256]{0:T(256)} %param.9) | copy-start | bytes 3076
where the time goes:
time: 89.3 us; the launch traced here: 89 us
  blocking collectives  72.2 us (81%)
  matrix products  13 us (15%)
  other arithmetic  2.54 us (3%)
  local copies, waits for them, and re-layouts  1.2 us (1%)
    all_to_all x2, blocking collectives, joined_exchange(): lax.all_to_all(blocks, axis, split_axis=0, concat_axis=0, tiled=True)  72.2 us
    dot_general x1, matrix products, local(): jnp.dot(rows, w_in[0], preferred_element_type=jnp.float32)  5.23 us
    dot_general x1, matrix products, local(): lax.dot_general(hidden, w_out[0], (((1,), (1,)), ((), ())), preferred_ele...  4.97 us

commit v1 on v0

v1 whole, which is shorter than its diff:
```python
import jax
import jax.numpy as jnp
from jax import lax
from jax.experimental import pallas as pl
from jax.experimental.pallas import tpu as pltpu
from jax.sharding import PartitionSpec as P

AXES = ("expert", "tensor")
CAP = 2
VMEM = pl.BlockSpec(memory_space=pltpu.VMEM)
HBM = pl.BlockSpec(memory_space=pltpu.HBM)
MIB = 2**20


def slot_index(ids_ref, slots_ref):
    slots = slots_ref[...]
    return jnp.where(slots >= 0, ids_ref[...] * CAP + slots, -1)


def dispatch_kernel(
    tokens_hbm,
    gain_hbm,
    gates_hbm,
    ids_hbm,
    slots_hbm,
    w_in_hbm,
    sent_ref,
    tokens_ref,
    gates_ref,
    ids_ref,
    slots_ref,
    w_in_ref,
    gain_ref,
    sems,
):
    pairs = (
        (tokens_hbm, tokens_ref),
        (ids_hbm, ids_ref),
        (slots_hbm, slots_ref),
        (gain_hbm, gain_ref),
        (gates_hbm, gates_ref),
        (w_in_hbm, w_in_ref),
    )
    copies = [pltpu.make_async_copy(a, b, sems.at[i]) for i, (a, b) in enumerate(pairs)]
    for copy in copies:
        copy.start()
    for copy in copies[:5]:
        copy.wait()
    count, _, width = sent_ref.shape
    tok_dev = tokens_ref.shape[0]
    values = tokens_ref[...].astype(jnp.float32)
    square = jnp.mean(values * values, axis=-1, keepdims=True)
    normed = values * lax.rsqrt(square + 1e-06) * gain_ref[...][None, :]
    rows = lax.broadcasted_iota(jnp.int32, (count * CAP, tok_dev), 0)
    masked = (rows == slot_index(ids_ref, slots_ref)[None, :]).astype(jnp.float32)
    buffer = jnp.dot(
        masked.astype(jnp.bfloat16),
        normed.astype(jnp.bfloat16),
        preferred_element_type=jnp.float32,
    )
    sent_ref[...] = buffer.astype(jnp.bfloat16).reshape(count, CAP, width)
    copies[5].wait()


def in_hbm(array):
    return pltpu.with_memory_space_constraint(array, pltpu.HBM)


def dispatch(tokens, norm_gain, gates, expert_ids, slots, w_in, experts):
    tok_dev, width = tokens.shape
    return pl.pallas_call(
        dispatch_kernel,
        out_shape=(
            pltpu.VMEM((experts, CAP, width), jnp.bfloat16),
            *(pltpu.VMEM(a.shape, a.dtype) for a in (tokens, gates, expert_ids, slots, w_in)),
        ),
        in_specs=[HBM] * 6,
        out_specs=(VMEM,) * 6,
        scratch_shapes=[pltpu.VMEM(norm_gain.shape, jnp.float32), pltpu.SemaphoreType.DMA((6,))],
        compiler_params=pltpu.CompilerParams(vmem_limit_bytes=8 * MIB),
        cost_estimate=pl.CostEstimate(
            flops=2 * experts * CAP * tok_dev * width,
            bytes_accessed=2 * tok_dev * width + 2 * w_in.size,
            transcendentals=tok_dev,
        ),
        name="dispatch",
    )(*(in_hbm(a) for a in (tokens, norm_gain, gates, expert_ids, slots, w_in)))


def expert_kernel(rows_ref, w_in_ref, w_out_hbm, out_ref, hidden_ref, w_out_ref, sem):
    copy = pltpu.make_async_copy(w_out_hbm, w_out_ref, sem)
    copy.start()
    blocks, _, width = rows_ref.shape
    ff = w_in_ref.shape[-1]
    rows = rows_ref[...].reshape(blocks * CAP, width)
    tile = 512
    for at in range(0, ff, tile):
        part = jnp.dot(rows, w_in_ref[0, :, at : at + tile], preferred_element_type=jnp.float32)
        hidden_ref[:, at : at + tile] = jnp.maximum(part, 0.0).astype(jnp.bfloat16)
    copy.wait()
    tile = 256
    for at in range(0, width, tile):
        part = lax.dot_general(
            hidden_ref[...],
            w_out_ref[0, at : at + tile, :],
            (((1,), (1,)), ((), ())),
            preferred_element_type=jnp.float32,
        )
        out_ref[:, :, at : at + tile] = part.astype(jnp.bfloat16).reshape(blocks, CAP, tile)


def run_expert(rows, w_in, w_out):
    blocks, _, width = rows.shape
    ff = w_in.shape[-1]
    return pl.pallas_call(
        expert_kernel,
        out_shape=pltpu.VMEM(rows.shape, jnp.bfloat16),
        in_specs=[VMEM, VMEM, HBM],
        out_specs=VMEM,
        scratch_shapes=[
            pltpu.VMEM((blocks * CAP, ff), jnp.bfloat16),
            pltpu.VMEM(w_out.shape, w_out.dtype),
            pltpu.SemaphoreType.DMA,
        ],
        compiler_params=pltpu.CompilerParams(vmem_limit_bytes=24 * MIB),
        cost_estimate=pl.CostEstimate(
            flops=4 * blocks * CAP * width * ff, bytes_accessed=4 * width * ff, transcendentals=0
        ),
        name="expert_ffn",
    )(rows, w_in, in_hbm(w_out))


def combine_kernel(returned_ref, tokens_ref, gates_ref, ids_ref, slots_ref, mixed_ref):
    experts, _, width = returned_ref.shape
    tok_dev = tokens_ref.shape[0]
    columns = lax.broadcasted_iota(jnp.int32, (tok_dev, experts * CAP), 1)
    masked = (columns == slot_index(ids_ref, slots_ref).reshape(tok_dev, 1)).astype(jnp.float32)
    picked = jnp.dot(
        masked.astype(jnp.bfloat16),
        returned_ref[...].reshape(experts * CAP, width),
        preferred_element_type=jnp.float32,
    )
    gates = gates_ref[...].reshape(tok_dev, 1)
    mixed_ref[...] = (tokens_ref[...].astype(jnp.float32) + gates * picked).astype(jnp.bfloat16)


def combine(returned, tokens, gates, expert_ids, slots):
    experts, _, width = returned.shape
    tok_dev = tokens.shape[0]
    return pl.pallas_call(
        combine_kernel,
        out_shape=jax.ShapeDtypeStruct(tokens.shape, jnp.bfloat16),
        in_specs=[VMEM] * 5,
        out_specs=VMEM,
        compiler_params=pltpu.CompilerParams(vmem_limit_bytes=8 * MIB),
        cost_estimate=pl.CostEstimate(
            flops=2 * experts * CAP * tok_dev * width,
            bytes_accessed=2 * tok_dev * width,
            transcendentals=0,
        ),
        name="combine",
    )(returned, tokens, gates, expert_ids, slots)


def exchange(blocks):
    return lax.all_to_all(blocks, AXES, 0, 0, tiled=True)


def local(tokens, norm_gain, gates, expert_ids, slots, w_in, w_out):
    experts = lax.axis_size("expert") * lax.axis_size("tensor")
    sent, *kept, near_w_in = dispatch(tokens, norm_gain, gates, expert_ids, slots, w_in, experts)
    result = run_expert(exchange(sent), near_w_in, w_out)
    return combine(exchange(result), *kept)


def solution(mesh):
    rows = P(AXES)
    matrix = P(AXES, None)
    weights = P(AXES, None, None)
    return jax.shard_map(
        local,
        mesh=mesh,
        in_specs=(matrix, P(), rows, rows, rows, weights, weights),
        out_specs=matrix,
        check_vma=False,
    )
```

time: 89.3 us -> 85 us (0.952)
  matrix products: 13 us -> 0 us
  Pallas kernels: 0 us -> 12.6 us
  other arithmetic: 2.54 us -> 0 us
  local copies, waits for them, and re-layouts: 1.2 us -> 0 us
    dot_general x4 -> x0, matrix products: 13 us -> none  [the longest x1 5.23 us: local(): jnp.dot(rows, w_in[0], preferred_element_type=jnp.float32)]
    pallas_call x0 -> x3, Pallas kernels: none -> 12.6 us  [the longest x1 8.87 us: run_expert(): pl.pallas_call(expert_kernel, out_shape=pltpu.VMEM(rows.shape, jnp.bfloat...]
    another operation x4 -> x0, local copies, waits for them, and re-layouts: 1.18 us -> none  [the longest x2 0.59 us: joined_exchange(): blocks = blocks.reshape(-1, *inside)]
    reduce_sum x1 -> x0, other arithmetic: 1.15 us -> none  [normalize(): square = jnp.mean(values * values, axis=-1, keepdims=True)]
where the time goes in v1:
time: 85 us; the launch traced here: 84.8 us
  blocking collectives  72.2 us (85%)
  Pallas kernels  12.6 us (15%)
    all_to_all x2, blocking collectives, exchange(): return lax.all_to_all(blocks, AXES, 0, 0, tiled=True)  72.2 us
    pallas_call x1, Pallas kernels, run_expert(): pl.pallas_call(expert_kernel, out_shape=pltpu.VMEM(rows.shape, jnp.bfloat...  8.87 us
    pallas_call x1, Pallas kernels, dispatch(): pl.pallas_call(dispatch_kernel, out_shape=(pltpu.VMEM((experts, CAP, widt...  2.58 us

profile of v1, /device:TPU:1, one launch (start us, length us, event | category | flops | bytes accessed | tf_op | source)
XLA Modules:
  0.0 84.8 jit_solution(12250583656201674069)
XLA Ops:
  0.0 2.6 %dispatch.1 = (bf16[256,2,768]{2,1,0:T(2,128)(2,1)S(1)}, bf16[256,768]{1,0:T(8,128)(2,1)S(1)}, f32[256]{0:T(256)S(1)}, s32[256]{0:T(256)S(1)}, s32[256]{0:T(256)S(1)}, /*index=5*/bf16[1,768,3072]{2,1,0:T(8,128)(2,1)S(1)}) custom-call(bf16[256,768]{1,0:T(8,128)(2,1)} %tokens_hbm.1, f32[768]{0:T(1024)} %gain_hbm.1, f32[256]{0:T(256)} %gates_hbm.1, ...), custom_call_target="tpu_custom_call" | custom-call | flops 201326592 | bytes 5111808 | tf_op jit(solution)/shard_map/dispatch/pallas_call | solution.py:71
  2.6 40.9 %all_to_all.10.rows_ref = bf16[256,2,768]{2,1,0:T(2,128)(2,1)S(1)} all-to-all(bf16[256,2,768]{2,1,0:T(2,128)(2,1)S(1)} %get-tuple-element.11), channel_id=1, replica_groups=mesh['expert'=128,'tensor'=2] {'expert','tensor'}, dimensions={0} | all-to-all | bytes 1572864 | tf_op jit(solution)/shard_map/all_to_all | solution.py:166
  43.5 8.9 %expert_ffn.1 = bf16[256,2,768]{2,1,0:T(2,128)(2,1)S(1)} custom-call(bf16[256,2,768]{2,1,0:T(2,128)(2,1)S(1)} %all_to_all.10.rows_ref, bf16[1,768,3072]{2,1,0:T(8,128)(2,1)S(1)} %get-tuple-element.12.w_in_ref, bf16[1,768,3072]{2,1,0:T(8,128)(2,1)} %w_out_hbm.1), custom_call_target="tpu_custom_call" | custom-call | flops 4831838208 | bytes 9437184 | tf_op jit(solution)/shard_map/expert_ffn/pallas_call | solution.py:115
  52.3 31.3 %all_to_all.11.returned_ref = bf16[256,2,768]{2,1,0:T(2,128)(2,1)S(1)} all-to-all(bf16[256,2,768]{2,1,0:T(2,128)(2,1)S(1)} %expert_ffn.1), channel_id=1, replica_groups=mesh['expert'=128,'tensor'=2] {'expert','tensor'}, dimensions={0} | all-to-all | bytes 1572864 | tf_op jit(solution)/shard_map/all_to_all | solution.py:166
  83.6 1.2 %combine.1 = bf16[256,768]{1,0:T(8,128)(2,1)} custom-call(bf16[256,2,768]{2,1,0:T(2,128)(2,1)S(1)} %all_to_all.11.returned_ref, bf16[256,768]{1,0:T(8,128)(2,1)S(1)} %get-tuple-element.13.tokens_ref, f32[256]{0:T(256)S(1)} %get-tuple-element.14.gates_ref, s32[256]{0:T(256)S(1)} %get-tuple-element.15.ids_ref, s32[256]{0:T(256)S(1)} %get-tuple-element.16.slots_ref), custom_call_target="tpu_custom_call" | custom-call | flops 201326592 | bytes 393216 | tf_op jit(solution)/shard_map/combine/pallas_call | solution.py:150

commit v2 on v1

--- a/solution.py
+++ b/solution.py
@@ -87,16 +87,22 @@
     )(*(in_hbm(a) for a in (tokens, norm_gain, gates, expert_ids, slots, w_in)))
 
 
-def expert_kernel(rows_ref, w_in_ref, w_out_hbm, out_ref, hidden_ref, w_out_ref, sem):
+def expert_kernel(rows_ref, w_in_ref, w_out_hbm, out_ref, flat_ref, hidden_ref, w_out_ref, sem):
     copy = pltpu.make_async_copy(w_out_hbm, w_out_ref, sem)
     copy.start()
     blocks, _, width = rows_ref.shape
     ff = w_in_ref.shape[-1]
-    rows = rows_ref[...].reshape(blocks * CAP, width)
-    tile = 512
-    for at in range(0, ff, tile):
-        part = jnp.dot(rows, w_in_ref[0, :, at : at + tile], preferred_element_type=jnp.float32)
-        hidden_ref[:, at : at + tile] = jnp.maximum(part, 0.0).astype(jnp.bfloat16)
+    flat_ref[...] = rows_ref[...].reshape(blocks * CAP, width)
+    tile = ff // 2
+
+    @pl.loop(0, ff // tile)
+    def _(step):
+        at = pl.multiple_of(step * tile, tile)
+        part = jnp.dot(
+            flat_ref[...], w_in_ref[0, :, pl.ds(at, tile)], preferred_element_type=jnp.float32
+        )
+        hidden_ref[:, pl.ds(at, tile)] = jnp.maximum(part, 0.0).astype(jnp.bfloat16)
+
     copy.wait()
     tile = 256
     for at in range(0, width, tile):
@@ -118,6 +124,7 @@
         in_specs=[VMEM, VMEM, HBM],
         out_specs=VMEM,
         scratch_shapes=[
+            pltpu.VMEM((blocks * CAP, width), jnp.bfloat16),
             pltpu.VMEM((blocks * CAP, ff), jnp.bfloat16),
             pltpu.VMEM(w_out.shape, w_out.dtype),
             pltpu.SemaphoreType.DMA,

time: 85 us -> 81.7 us (0.961)
  Pallas kernels: 12.6 us -> 9.38 us
    pallas_call x1, Pallas kernels: 8.87 us -> 5.61 us  [run_expert(): pl.pallas_call(expert_kernel, out_shape=pltpu.VMEM(rows.shape, jnp.bfloat...]
where the time goes in v2:
time: 81.7 us; the launch traced here: 81.6 us
  blocking collectives  72.2 us (88%)
  Pallas kernels  9.38 us (11%)
    all_to_all x2, blocking collectives, exchange(): return lax.all_to_all(blocks, AXES, 0, 0, tiled=True)  72.2 us
    pallas_call x1, Pallas kernels, run_expert(): pl.pallas_call(expert_kernel, out_shape=pltpu.VMEM(rows.shape, jnp.bfloat...  5.61 us
    pallas_call x1, Pallas kernels, dispatch(): pl.pallas_call(dispatch_kernel, out_shape=(pltpu.VMEM((experts, CAP, widt...  2.58 us

profile of v2, /device:TPU:1, one launch (start us, length us, event | category | flops | bytes accessed | tf_op | source)
XLA Modules:
  0.0 81.6 jit_solution(8833612468255289915)
XLA Ops:
  0.0 2.6 %dispatch.1 = (bf16[256,2,768]{2,1,0:T(2,128)(2,1)S(1)}, bf16[256,768]{1,0:T(8,128)(2,1)S(1)}, f32[256]{0:T(256)S(1)}, s32[256]{0:T(256)S(1)}, s32[256]{0:T(256)S(1)}, /*index=5*/bf16[1,768,3072]{2,1,0:T(8,128)(2,1)S(1)}) custom-call(bf16[256,768]{1,0:T(8,128)(2,1)} %tokens_hbm.1, f32[768]{0:T(1024)} %gain_hbm.1, f32[256]{0:T(256)} %gates_hbm.1, ...), custom_call_target="tpu_custom_call" | custom-call | flops 201326592 | bytes 5111808 | tf_op jit(solution)/shard_map/dispatch/pallas_call | solution.py:71
  2.6 40.9 %all_to_all.10.rows_ref = bf16[256,2,768]{2,1,0:T(2,128)(2,1)S(1)} all-to-all(bf16[256,2,768]{2,1,0:T(2,128)(2,1)S(1)} %get-tuple-element.11), channel_id=1, replica_groups=mesh['expert'=128,'tensor'=2] {'expert','tensor'}, dimensions={0} | all-to-all | bytes 1572864 | tf_op jit(solution)/shard_map/all_to_all | solution.py:173
  43.5 5.6 %expert_ffn.1 = bf16[256,2,768]{2,1,0:T(2,128)(2,1)S(1)} custom-call(bf16[256,2,768]{2,1,0:T(2,128)(2,1)S(1)} %all_to_all.10.rows_ref, bf16[1,768,3072]{2,1,0:T(8,128)(2,1)S(1)} %get-tuple-element.12.w_in_ref, bf16[1,768,3072]{2,1,0:T(8,128)(2,1)} %w_out_hbm.1), custom_call_target="tpu_custom_call" | custom-call | flops 4831838208 | bytes 9437184 | tf_op jit(solution)/shard_map/expert_ffn/pallas_call | solution.py:121
  49.1 31.3 %all_to_all.11.returned_ref = bf16[256,2,768]{2,1,0:T(2,128)(2,1)S(1)} all-to-all(bf16[256,2,768]{2,1,0:T(2,128)(2,1)S(1)} %expert_ffn.1), channel_id=1, replica_groups=mesh['expert'=128,'tensor'=2] {'expert','tensor'}, dimensions={0} | all-to-all | bytes 1572864 | tf_op jit(solution)/shard_map/all_to_all | solution.py:173
  80.4 1.2 %combine.1 = bf16[256,768]{1,0:T(8,128)(2,1)} custom-call(bf16[256,2,768]{2,1,0:T(2,128)(2,1)S(1)} %all_to_all.11.returned_ref, bf16[256,768]{1,0:T(8,128)(2,1)S(1)} %get-tuple-element.13.tokens_ref, f32[256]{0:T(256)S(1)} %get-tuple-element.14.gates_ref, s32[256]{0:T(256)S(1)} %get-tuple-element.15.ids_ref, s32[256]{0:T(256)S(1)} %get-tuple-element.16.slots_ref), custom_call_target="tpu_custom_call" | custom-call | flops 201326592 | bytes 393216 | tf_op jit(solution)/shard_map/combine/pallas_call | solution.py:157

commit v3 on v2

v3 whole, which is shorter than its diff:
```python
import jax
import jax.numpy as jnp
from jax import lax
from jax.experimental import pallas as pl
from jax.experimental.pallas import tpu as pltpu
from jax.sharding import PartitionSpec as P

AXES = ("expert", "tensor")
CAP = 2
HALVES = 2
RETURN_ORDER = (0, 4, 5, 6, 7, 1, 2, 3)
VMEM = pl.BlockSpec(memory_space=pltpu.VMEM)
HBM = pl.BlockSpec(memory_space=pltpu.HBM)
MIB = 2**20


def slot_index(owners, slots_ref):
    slots = slots_ref[...]
    return jnp.where(slots >= 0, owners * CAP + slots, -1)


def return_position(ids, experts):
    span = experts // len(RETURN_ORDER)
    shift = jnp.zeros_like(ids)
    for at, group in enumerate(RETURN_ORDER):
        inside = (ids >= group * span) & (ids < (group + 1) * span)
        shift = jnp.where(inside, (at - group) * span, shift)
    return ids + shift


def return_group(experts):
    span = experts // len(RETURN_ORDER)
    return [group * span + i for group in RETURN_ORDER for i in range(span)]


def dispatch_kernel(
    tokens_hbm,
    gain_hbm,
    gates_hbm,
    ids_hbm,
    slots_hbm,
    w_in_hbm,
    sent_ref,
    tokens_ref,
    gates_ref,
    ids_ref,
    slots_ref,
    w_in_ref,
    gain_ref,
    sems,
):
    pairs = (
        (tokens_hbm, tokens_ref),
        (ids_hbm, ids_ref),
        (slots_hbm, slots_ref),
        (gain_hbm, gain_ref),
        (gates_hbm, gates_ref),
        (w_in_hbm.at[0, :, : w_in_ref.shape[-1]], w_in_ref.at[0]),
    )
    copies = [pltpu.make_async_copy(a, b, sems.at[i]) for i, (a, b) in enumerate(pairs)]
    for copy in copies:
        copy.start()
    for copy in copies[:5]:
        copy.wait()
    count, _, width = sent_ref.shape
    tok_dev = tokens_ref.shape[0]
    values = tokens_ref[...].astype(jnp.float32)
    square = jnp.mean(values * values, axis=-1, keepdims=True)
    normed = values * lax.rsqrt(square + 1e-06) * gain_ref[...][None, :]
    rows = lax.broadcasted_iota(jnp.int32, (count * CAP, tok_dev), 0)
    masked = (rows == slot_index(ids_ref[...], slots_ref)[None, :]).astype(jnp.float32)
    buffer = jnp.dot(
        masked.astype(jnp.bfloat16),
        normed.astype(jnp.bfloat16),
        preferred_element_type=jnp.float32,
    )
    sent_ref[...] = buffer.astype(jnp.bfloat16).reshape(count, CAP, width)
    copies[5].wait()


def in_hbm(array):
    return pltpu.with_memory_space_constraint(array, pltpu.HBM)


def dispatch(tokens, norm_gain, gates, expert_ids, slots, w_in, experts):
    tok_dev, width = tokens.shape
    return pl.pallas_call(
        dispatch_kernel,
        out_shape=(
            pltpu.VMEM((experts, CAP, width), jnp.bfloat16),
            *(pltpu.VMEM(a.shape, a.dtype) for a in (tokens, gates, expert_ids, slots)),
            pltpu.VMEM((HALVES, width, w_in.shape[-1] // HALVES), w_in.dtype),
        ),
        in_specs=[HBM] * 6,
        out_specs=(VMEM,) * 6,
        scratch_shapes=[pltpu.VMEM(norm_gain.shape, jnp.float32), pltpu.SemaphoreType.DMA((6,))],
        compiler_params=pltpu.CompilerParams(vmem_limit_bytes=8 * MIB),
        cost_estimate=pl.CostEstimate(
            flops=2 * experts * CAP * tok_dev * width,
            bytes_accessed=2 * tok_dev * width + 2 * w_in.size,
            transcendentals=tok_dev,
        ),
        name="dispatch",
    )(*(in_hbm(a) for a in (tokens, norm_gain, gates, expert_ids, slots, w_in)))


def expert_kernel(
    rows_ref, _, w_in_hbm, w_out_hbm, out_ref, w_in_ref, flat_ref, hidden_ref, w_out_ref, sems
):
    blocks, _, width = rows_ref.shape
    tile = w_in_ref.shape[-1]
    out_tile = 256
    outs = range(0, width, out_tile)
    late = [
        pltpu.make_async_copy(
            w_in_hbm.at[0, :, half * tile : (half + 1) * tile], w_in_ref.at[half], sems.at[half]
        )
        for half in range(1, HALVES)
    ]
    lasts = [
        pltpu.make_async_copy(
            w_out_hbm.at[0, at : at + out_tile], w_out_ref.at[at : at + out_tile], sems.at[HALVES + i]
        )
        for i, at in enumerate(outs)
    ]
    for copy in late + lasts:
        copy.start()
    span = blocks // len(RETURN_ORDER)
    for at, group in enumerate(RETURN_ORDER):
        rows = rows_ref[group * span : (group + 1) * span].reshape(span * CAP, width)
        flat_ref[at * span * CAP : (at + 1) * span * CAP] = rows

    @pl.loop(0, HALVES)
    def _(step):
        for half in range(1, HALVES):

            @pl.when(step == half)
            def _():
                late[half - 1].wait()

        part = jnp.dot(flat_ref[...], w_in_ref[step], preferred_element_type=jnp.float32)
        at = pl.multiple_of(step * tile, tile)
        hidden_ref[:, pl.ds(at, tile)] = jnp.maximum(part, 0.0).astype(jnp.bfloat16)

    for copy in lasts:
        copy.wait()
    for at in outs:
        part = lax.dot_general(
            hidden_ref[...],
            w_out_ref[at : at + out_tile],
            (((1,), (1,)), ((), ())),
            preferred_element_type=jnp.float32,
        )
        out_ref[:, :, at : at + out_tile] = part.astype(jnp.bfloat16).reshape(blocks, CAP, out_tile)


def run_expert(rows, near_w_in, w_in, w_out):
    blocks, _, width = rows.shape
    ff = w_in.shape[-1]
    return pl.pallas_call(
        expert_kernel,
        out_shape=(
            pltpu.VMEM(rows.shape, jnp.bfloat16),
            pltpu.VMEM(near_w_in.shape, near_w_in.dtype),
        ),
        in_specs=[VMEM, VMEM, HBM, HBM],
        out_specs=(VMEM, VMEM),
        input_output_aliases={1: 1},
        scratch_shapes=[
            pltpu.VMEM((blocks * CAP, width), jnp.bfloat16),
            pltpu.VMEM((blocks * CAP, ff), jnp.bfloat16),
            pltpu.VMEM((width, ff), w_out.dtype),
            pltpu.SemaphoreType.DMA((HALVES + 3,)),
        ],
        compiler_params=pltpu.CompilerParams(vmem_limit_bytes=24 * MIB),
        cost_estimate=pl.CostEstimate(
            flops=4 * blocks * CAP * width * ff, bytes_accessed=4 * width * ff, transcendentals=0
        ),
        name="expert_ffn",
    )(rows, near_w_in, in_hbm(w_in), in_hbm(w_out))[0]


def combine_kernel(
    returned_ref, tokens_ref, gates_ref, ids_ref, slots_ref, mixed_hbm, mixed_ref, sems
):
    experts, _, width = returned_ref.shape
    tok_dev = tokens_ref.shape[0]
    owners = return_position(ids_ref[...], experts)
    index = slot_index(owners, slots_ref).reshape(tok_dev, 1)
    gates = gates_ref[...].reshape(tok_dev, 1)
    returned = returned_ref[...].reshape(experts * CAP, width)
    part = tok_dev // 2
    columns = lax.broadcasted_iota(jnp.int32, (part, experts * CAP), 1)
    copies = []
    for at in range(0, tok_dev, part):
        rows = slice(at, at + part)
        masked = (columns == index[rows]).astype(jnp.float32).astype(jnp.bfloat16)
        picked = jnp.dot(masked, returned, preferred_element_type=jnp.float32)
        mixed = tokens_ref[rows].astype(jnp.float32) + gates[rows] * picked
        mixed_ref[rows] = mixed.astype(jnp.bfloat16)
        copy = pltpu.make_async_copy(mixed_ref.at[rows], mixed_hbm.at[rows], sems.at[at // part])
        copy.start()
        copies.append(copy)
    for copy in copies:
        copy.wait()


def combine(returned, tokens, gates, expert_ids, slots):
    experts, _, width = returned.shape
    tok_dev = tokens.shape[0]
    return pl.pallas_call(
        combine_kernel,
        out_shape=jax.ShapeDtypeStruct(tokens.shape, jnp.bfloat16),
        in_specs=[VMEM] * 5,
        out_specs=HBM,
        scratch_shapes=[
            pltpu.VMEM(tokens.shape, jnp.bfloat16),
            pltpu.SemaphoreType.DMA((2,)),
        ],
        compiler_params=pltpu.CompilerParams(vmem_limit_bytes=8 * MIB),
        cost_estimate=pl.CostEstimate(
            flops=2 * experts * CAP * tok_dev * width,
            bytes_accessed=2 * tok_dev * width,
            transcendentals=0,
        ),
        name="combine",
    )(returned, tokens, gates, expert_ids, slots)


def exchange(blocks, groups=None):
    return lax.all_to_all(blocks, AXES, 0, 0, tiled=True, axis_index_groups=groups)


def local(tokens, norm_gain, gates, expert_ids, slots, w_in, w_out):
    experts = lax.axis_size("expert") * lax.axis_size("tensor")
    sent, *kept, near_w_in = dispatch(tokens, norm_gain, gates, expert_ids, slots, w_in, experts)
    result = run_expert(exchange(sent), near_w_in, w_in, w_out)
    return combine(exchange(result, [return_group(experts)]), *kept)


def solution(mesh):
    rows = P(AXES)
    matrix = P(AXES, None)
    weights = P(AXES, None, None)
    return jax.shard_map(
        local,
        mesh=mesh,
        in_specs=(matrix, P(), rows, rows, rows, weights, weights),
        out_specs=matrix,
        check_vma=False,
    )
```

time: 81.7 us -> 80.1 us (0.980)
  blocking collectives: 72.2 us -> 70.5 us
    all_to_all x2, blocking collectives: 72.2 us -> 70.5 us  [exchange(): lax.all_to_all(blocks, AXES, 0, 0, tiled=True, axis_index_groups=groups)]
where the time goes in v3:
time: 80.1 us; the launch traced here: 79.3 us
  blocking collectives  70.5 us (88%)
  Pallas kernels  8.82 us (11%)
    all_to_all x2, blocking collectives, exchange(): lax.all_to_all(blocks, AXES, 0, 0, tiled=True, axis_index_groups=groups)  70.5 us
    pallas_call x1, Pallas kernels, run_expert(): pl.pallas_call(expert_kernel, out_shape=(pltpu.VMEM(rows.shape, jnp.bfloa...  5.76 us
    pallas_call x1, Pallas kernels, dispatch(): pl.pallas_call(dispatch_kernel, out_shape=(pltpu.VMEM((experts, CAP, widt...  1.92 us

profile of v3, /device:TPU:1, one launch (start us, length us, event | category | flops | bytes accessed | tf_op | source)
XLA Modules:
  0.0 79.3 jit_solution(6414316872472831677)
XLA Ops:
  0.0 1.9 %dispatch.1 = (bf16[256,2,768]{2,1,0:T(2,128)(2,1)S(1)}, bf16[256,768]{1,0:T(8,128)(2,1)S(1)}, f32[256]{0:T(256)S(1)}, s32[256]{0:T(256)S(1)}, s32[256]{0:T(256)S(1)}, /*index=5*/bf16[2,768,1536]{2,1,0:T(8,128)(2,1)S(1)}) custom-call(bf16[256,768]{1,0:T(8,128)(2,1)} %tokens_hbm.1, f32[768]{0:T(1024)} %gain_hbm.1, f32[256]{0:T(256)} %gates_hbm.1, ...), custom_call_target="tpu_custom_call" | custom-call | flops 201326592 | bytes 5111808 | tf_op jit(solution)/shard_map/dispatch/pallas_call | solution.py:87
  1.9 40.9 %all_to_all.10.rows_ref = bf16[256,2,768]{2,1,0:T(2,128)(2,1)S(1)} all-to-all(bf16[256,2,768]{2,1,0:T(2,128)(2,1)S(1)} %get-tuple-element.12), channel_id=1, replica_groups=mesh['expert'=128,'tensor'=2] {'expert','tensor'}, dimensions={0} | all-to-all | bytes 1572864 | tf_op jit(solution)/shard_map/all_to_all | solution.py:231
  42.8 5.8 %expert_ffn.1 = (bf16[256,2,768]{2,1,0:T(2,128)(2,1)S(1)}, bf16[2,768,1536]{2,1,0:T(8,128)(2,1)S(1)}) custom-call(bf16[256,2,768]{2,1,0:T(2,128)(2,1)S(1)} %all_to_all.10.rows_ref, bf16[2,768,1536]{2,1,0:T(8,128)(2,1)S(1)} %get-tuple-element.13._, bf16[1,768,3072]{2,1,0:T(8,128)(2,1)} %w_in_hbm.3, ...), custom_call_target="tpu_custom_call", output_to_operand_aliasing={{1}: (1, {})} | custom-call | flops 4831838208 | bytes 9437184 | tf_op jit(solution)/shard_map/expert_ffn/pallas_call | solution.py:160
  48.6 29.6 %all_to_all.11.returned_ref = bf16[256,2,768]{2,1,0:T(2,128)(2,1)S(1)} all-to-all(bf16[256,2,768]{2,1,0:T(2,128)(2,1)S(1)} %get-tuple-element.14), channel_id=1, replica_groups={{0,1,2,3,4,5,6,7,8,9,10,11,12,13,14,15,16,17,18,19,20,21,22,23,24,25,26..., dimensions={0} | all-to-all | bytes 1572864 | tf_op jit(solution)/shard_map/all_to_all | solution.py:231
  78.2 1.1 %combine.1 = bf16[256,768]{1,0:T(8,128)(2,1)} custom-call(bf16[256,2,768]{2,1,0:T(2,128)(2,1)S(1)} %all_to_all.11.returned_ref, bf16[256,768]{1,0:T(8,128)(2,1)S(1)} %get-tuple-element.15.tokens_ref, f32[256]{0:T(256)S(1)} %get-tuple-element.16.gates_ref, s32[256]{0:T(256)S(1)} %get-tuple-element.17.ids_ref, s32[256]{0:T(256)S(1)} %get-tuple-element.18.slots_ref), custom_call_target="tpu_custom_call" | custom-call | flops 201326592 | bytes 393216 | tf_op jit(solution)/shard_map/combine/pallas_call | solution.py:211

commit v4 on v3

--- a/solution.py
+++ b/solution.py
@@ -8,6 +8,7 @@
 AXES = ("expert", "tensor")
 CAP = 2
 HALVES = 2
+DISPATCH_ORDER = (0, 1, 4, 2, 6, 5, 7, 3)
 RETURN_ORDER = (0, 4, 5, 6, 7, 1, 2, 3)
 VMEM = pl.BlockSpec(memory_space=pltpu.VMEM)
 HBM = pl.BlockSpec(memory_space=pltpu.HBM)
@@ -19,18 +20,18 @@
     return jnp.where(slots >= 0, owners * CAP + slots, -1)
 
 
-def return_position(ids, experts):
-    span = experts // len(RETURN_ORDER)
+def position_of(ids, order, experts):
+    span = experts // len(order)
     shift = jnp.zeros_like(ids)
-    for at, group in enumerate(RETURN_ORDER):
+    for at, group in enumerate(order):
         inside = (ids >= group * span) & (ids < (group + 1) * span)
         shift = jnp.where(inside, (at - group) * span, shift)
     return ids + shift
 
 
-def return_group(experts):
-    span = experts // len(RETURN_ORDER)
-    return [group * span + i for group in RETURN_ORDER for i in range(span)]
+def members(order, experts):
+    span = experts // len(order)
+    return [group * span + i for group in order for i in range(span)]
 
 
 def dispatch_kernel(
@@ -68,7 +69,8 @@
     square = jnp.mean(values * values, axis=-1, keepdims=True)
     normed = values * lax.rsqrt(square + 1e-06) * gain_ref[...][None, :]
     rows = lax.broadcasted_iota(jnp.int32, (count * CAP, tok_dev), 0)
-    masked = (rows == slot_index(ids_ref[...], slots_ref)[None, :]).astype(jnp.float32)
+    owners = position_of(ids_ref[...], DISPATCH_ORDER, count)
+    masked = (rows == slot_index(owners, slots_ref)[None, :]).astype(jnp.float32)
     buffer = jnp.dot(
         masked.astype(jnp.bfloat16),
         normed.astype(jnp.bfloat16),
@@ -127,7 +129,8 @@
         copy.start()
     span = blocks // len(RETURN_ORDER)
     for at, group in enumerate(RETURN_ORDER):
-        rows = rows_ref[group * span : (group + 1) * span].reshape(span * CAP, width)
+        came = DISPATCH_ORDER.index(group) * span
+        rows = rows_ref[came : came + span].reshape(span * CAP, width)
         flat_ref[at * span * CAP : (at + 1) * span * CAP] = rows
 
     @pl.loop(0, HALVES)
@@ -185,7 +188,7 @@
 ):
     experts, _, width = returned_ref.shape
     tok_dev = tokens_ref.shape[0]
-    owners = return_position(ids_ref[...], experts)
+    owners = position_of(ids_ref[...], RETURN_ORDER, experts)
     index = slot_index(owners, slots_ref).reshape(tok_dev, 1)
     gates = gates_ref[...].reshape(tok_dev, 1)
     returned = returned_ref[...].reshape(experts * CAP, width)
@@ -227,15 +230,16 @@
     )(returned, tokens, gates, expert_ids, slots)
 
 
-def exchange(blocks, groups=None):
+def exchange(blocks, order):
+    groups = [members(order, blocks.shape[0])]
     return lax.all_to_all(blocks, AXES, 0, 0, tiled=True, axis_index_groups=groups)
 
 
 def local(tokens, norm_gain, gates, expert_ids, slots, w_in, w_out):
     experts = lax.axis_size("expert") * lax.axis_size("tensor")
     sent, *kept, near_w_in = dispatch(tokens, norm_gain, gates, expert_ids, slots, w_in, experts)
-    result = run_expert(exchange(sent), near_w_in, w_in, w_out)
-    return combine(exchange(result, [return_group(experts)]), *kept)
+    result = run_expert(exchange(sent, DISPATCH_ORDER), near_w_in, w_in, w_out)
+    return combine(exchange(result, RETURN_ORDER), *kept)
 
 
 def solution(mesh):

time: 80.1 us -> 79.8 us (level)
  no operation moved by 1% of the time
where the time goes in v4:
time: 79.8 us; the launch traced here: 79 us
  blocking collectives  70.2 us (88%)
  Pallas kernels  8.82 us (11%)
    all_to_all x2, blocking collectives, exchange(): lax.all_to_all(blocks, AXES, 0, 0, tiled=True, axis_index_groups=groups)  70.2 us
    pallas_call x1, Pallas kernels, run_expert(): pl.pallas_call(expert_kernel, out_shape=(pltpu.VMEM(rows.shape, jnp.bfloa...  5.77 us
    pallas_call x1, Pallas kernels, dispatch(): pl.pallas_call(dispatch_kernel, out_shape=(pltpu.VMEM((experts, CAP, widt...  1.92 us

profile of v4, /device:TPU:1, one launch (start us, length us, event | category | flops | bytes accessed | tf_op | source)
XLA Modules:
  0.0 79.0 jit_solution(5642750819886482847)
XLA Ops:
  0.0 1.9 %dispatch.1 = (bf16[256,2,768]{2,1,0:T(2,128)(2,1)S(1)}, bf16[256,768]{1,0:T(8,128)(2,1)S(1)}, f32[256]{0:T(256)S(1)}, s32[256]{0:T(256)S(1)}, s32[256]{0:T(256)S(1)}, /*index=5*/bf16[2,768,1536]{2,1,0:T(8,128)(2,1)S(1)}) custom-call(bf16[256,768]{1,0:T(8,128)(2,1)} %tokens_hbm.1, f32[768]{0:T(1024)} %gain_hbm.1, f32[256]{0:T(256)} %gates_hbm.1, ...), custom_call_target="tpu_custom_call" | custom-call | flops 201326592 | bytes 5111808 | tf_op jit(solution)/shard_map/dispatch/pallas_call | solution.py:89
  1.9 40.7 %all_to_all.10.rows_ref = bf16[256,2,768]{2,1,0:T(2,128)(2,1)S(1)} all-to-all(bf16[256,2,768]{2,1,0:T(2,128)(2,1)S(1)} %get-tuple-element.12), channel_id=1, replica_groups={{0,1,2,3,4,5,6,7,8,9,10,11,12,13,14,15,16,17,18,19,20,21,22,23,24,25,26..., dimensions={0} | all-to-all | bytes 1572864 | tf_op jit(solution)/shard_map/all_to_all | solution.py:235
  42.6 5.8 %expert_ffn.1 = (bf16[256,2,768]{2,1,0:T(2,128)(2,1)S(1)}, bf16[2,768,1536]{2,1,0:T(8,128)(2,1)S(1)}) custom-call(bf16[256,2,768]{2,1,0:T(2,128)(2,1)S(1)} %all_to_all.10.rows_ref, bf16[2,768,1536]{2,1,0:T(8,128)(2,1)S(1)} %get-tuple-element.13._, bf16[1,768,3072]{2,1,0:T(8,128)(2,1)} %w_in_hbm.3, ...), custom_call_target="tpu_custom_call", output_to_operand_aliasing={{1}: (1, {})} | custom-call | flops 4831838208 | bytes 9437184 | tf_op jit(solution)/shard_map/expert_ffn/pallas_call | solution.py:163
  48.4 29.5 %all_to_all.11.returned_ref = bf16[256,2,768]{2,1,0:T(2,128)(2,1)S(1)} all-to-all(bf16[256,2,768]{2,1,0:T(2,128)(2,1)S(1)} %get-tuple-element.14), channel_id=1, replica_groups={{0,1,2,3,4,5,6,7,8,9,10,11,12,13,14,15,16,17,18,19,20,21,22,23,24,25,26..., dimensions={0} | all-to-all | bytes 1572864 | tf_op jit(solution)/shard_map/all_to_all | solution.py:235
  77.9 1.1 %combine.1 = bf16[256,768]{1,0:T(8,128)(2,1)} custom-call(bf16[256,2,768]{2,1,0:T(2,128)(2,1)S(1)} %all_to_all.11.returned_ref, bf16[256,768]{1,0:T(8,128)(2,1)S(1)} %get-tuple-element.15.tokens_ref, f32[256]{0:T(256)S(1)} %get-tuple-element.16.gates_ref, s32[256]{0:T(256)S(1)} %get-tuple-element.17.ids_ref, s32[256]{0:T(256)S(1)} %get-tuple-element.18.slots_ref), custom_call_target="tpu_custom_call" | custom-call | flops 201326592 | bytes 393216 | tf_op jit(solution)/shard_map/combine/pallas_call | solution.py:214

commit v5 on v4

--- a/solution.py
+++ b/solution.py
@@ -8,6 +8,7 @@
 AXES = ("expert", "tensor")
 CAP = 2
 HALVES = 2
+LATE_PARTS = 1
 DISPATCH_ORDER = (0, 1, 4, 2, 6, 5, 7, 3)
 RETURN_ORDER = (0, 4, 5, 6, 7, 1, 2, 3)
 VMEM = pl.BlockSpec(memory_space=pltpu.VMEM)
@@ -113,18 +114,16 @@
     tile = w_in_ref.shape[-1]
     out_tile = 256
     outs = range(0, width, out_tile)
+    part_rows = width // LATE_PARTS
     late = [
         pltpu.make_async_copy(
-            w_in_hbm.at[0, :, half * tile : (half + 1) * tile], w_in_ref.at[half], sems.at[half]
+            w_in_hbm.at[0, at : at + part_rows, tile:],
+            w_in_ref.at[1, at : at + part_rows],
+            sems.at[at // part_rows],
         )
-        for half in range(1, HALVES)
+        for at in range(0, width, part_rows)
     ]
-    lasts = [
-        pltpu.make_async_copy(
-            w_out_hbm.at[0, at : at + out_tile], w_out_ref.at[at : at + out_tile], sems.at[HALVES + i]
-        )
-        for i, at in enumerate(outs)
-    ]
+    lasts = [pltpu.make_async_copy(w_out_hbm.at[0], w_out_ref, sems.at[LATE_PARTS])]
     for copy in late + lasts:
         copy.start()
     span = blocks // len(RETURN_ORDER)
@@ -135,11 +134,10 @@
 
     @pl.loop(0, HALVES)
     def _(step):
-        for half in range(1, HALVES):
-
-            @pl.when(step == half)
-            def _():
-                late[half - 1].wait()
+        @pl.when(step == 1)
+        def _():
+            for copy in late:
+                copy.wait()
 
         part = jnp.dot(flat_ref[...], w_in_ref[step], preferred_element_type=jnp.float32)
         at = pl.multiple_of(step * tile, tile)
@@ -173,7 +171,7 @@
             pltpu.VMEM((blocks * CAP, width), jnp.bfloat16),
             pltpu.VMEM((blocks * CAP, ff), jnp.bfloat16),
             pltpu.VMEM((width, ff), w_out.dtype),
-            pltpu.SemaphoreType.DMA((HALVES + 3,)),
+            pltpu.SemaphoreType.DMA((LATE_PARTS + 1,)),
         ],
         compiler_params=pltpu.CompilerParams(vmem_limit_bytes=24 * MIB),
         cost_estimate=pl.CostEstimate(

time: 79.8 us -> 79.8 us (level)
  no operation moved by 1% of the time
where the time goes in v5:
time: 79.8 us; the launch traced here: 79 us
  blocking collectives  70.2 us (88%)
  Pallas kernels  8.79 us (11%)
    all_to_all x2, blocking collectives, exchange(): lax.all_to_all(blocks, AXES, 0, 0, tiled=True, axis_index_groups=groups)  70.2 us
    pallas_call x1, Pallas kernels, run_expert(): pl.pallas_call(expert_kernel, out_shape=(pltpu.VMEM(rows.shape, jnp.bfloa...  5.73 us
    pallas_call x1, Pallas kernels, dispatch(): pl.pallas_call(dispatch_kernel, out_shape=(pltpu.VMEM((experts, CAP, widt...  1.92 us

profile of v5, /device:TPU:1, one launch (start us, length us, event | category | flops | bytes accessed | tf_op | source)
XLA Modules:
  0.0 79.0 jit_solution(10478146635016097784)
XLA Ops:
  0.0 1.9 %dispatch.1 = (bf16[256,2,768]{2,1,0:T(2,128)(2,1)S(1)}, bf16[256,768]{1,0:T(8,128)(2,1)S(1)}, f32[256]{0:T(256)S(1)}, s32[256]{0:T(256)S(1)}, s32[256]{0:T(256)S(1)}, /*index=5*/bf16[2,768,1536]{2,1,0:T(8,128)(2,1)S(1)}) custom-call(bf16[256,768]{1,0:T(8,128)(2,1)} %tokens_hbm.1, f32[768]{0:T(1024)} %gain_hbm.1, f32[256]{0:T(256)} %gates_hbm.1, ...), custom_call_target="tpu_custom_call" | custom-call | flops 201326592 | bytes 5111808 | tf_op jit(solution)/shard_map/dispatch/pallas_call | solution.py:90
  1.9 40.7 %all_to_all.10.rows_ref = bf16[256,2,768]{2,1,0:T(2,128)(2,1)S(1)} all-to-all(bf16[256,2,768]{2,1,0:T(2,128)(2,1)S(1)} %get-tuple-element.12), channel_id=1, replica_groups={{0,1,2,3,4,5,6,7,8,9,10,11,12,13,14,15,16,17,18,19,20,21,22,23,24,25,26..., dimensions={0} | all-to-all | bytes 1572864 | tf_op jit(solution)/shard_map/all_to_all | solution.py:233
  42.6 5.7 %expert_ffn.1 = (bf16[256,2,768]{2,1,0:T(2,128)(2,1)S(1)}, bf16[2,768,1536]{2,1,0:T(8,128)(2,1)S(1)}) custom-call(bf16[256,2,768]{2,1,0:T(2,128)(2,1)S(1)} %all_to_all.10.rows_ref, bf16[2,768,1536]{2,1,0:T(8,128)(2,1)S(1)} %get-tuple-element.13._, bf16[1,768,3072]{2,1,0:T(8,128)(2,1)} %w_in_hbm.3, ...), custom_call_target="tpu_custom_call", output_to_operand_aliasing={{1}: (1, {})} | custom-call | flops 4831838208 | bytes 9437184 | tf_op jit(solution)/shard_map/expert_ffn/pallas_call | solution.py:161
  48.4 29.5 %all_to_all.11.returned_ref = bf16[256,2,768]{2,1,0:T(2,128)(2,1)S(1)} all-to-all(bf16[256,2,768]{2,1,0:T(2,128)(2,1)S(1)} %get-tuple-element.14), channel_id=1, replica_groups={{0,1,2,3,4,5,6,7,8,9,10,11,12,13,14,15,16,17,18,19,20,21,22,23,24,25,26..., dimensions={0} | all-to-all | bytes 1572864 | tf_op jit(solution)/shard_map/all_to_all | solution.py:233
  77.9 1.1 %combine.1 = bf16[256,768]{1,0:T(8,128)(2,1)} custom-call(bf16[256,2,768]{2,1,0:T(2,128)(2,1)S(1)} %all_to_all.11.returned_ref, bf16[256,768]{1,0:T(8,128)(2,1)S(1)} %get-tuple-element.15.tokens_ref, f32[256]{0:T(256)S(1)} %get-tuple-element.16.gates_ref, s32[256]{0:T(256)S(1)} %get-tuple-element.17.ids_ref, s32[256]{0:T(256)S(1)} %get-tuple-element.18.slots_ref), custom_call_target="tpu_custom_call" | custom-call | flops 201326592 | bytes 393216 | tf_op jit(solution)/shard_map/combine/pallas_call | solution.py:212
